TPU v7x, 8 devices: a whole 2x2x1 slice. The times are simulated.
8 devices in a mesh: dp: 1 (over z), cz: 2 (over y), cy: 2 (over x), cx: 2 (over core).
Axes of the slice: x: 2, y: 2, z: 1, core: 2. Of those that a mesh axis runs over, the one named last changes fastest.
Arguments:
- x_tokens: bfloat16 [4096, 2048], P(('dp', 'cx', 'cz'), 'cy')
- w_up: bfloat16 [2048, 16384], P('cy', ('cz', 'cx'))
- w_down: bfloat16 [16384, 2048], P('cz', ('cy', 'cx'))
Outputs:
- output: bfloat16 [4096, 2048], P(('dp', 'cx', 'cz'), 'cy')
All inputs are finite; a program needn't handle non-finite values.
Results may differ from a plain program's by a relative error of at most 0.0114676.
Values are sent between devices in bfloat16 or wider.
A program may use at most 1 GiB of HBM per device.

v0:
```python
import jax
import jax.numpy as jnp
from jax import lax
from jax.experimental import pallas as pl
from jax.experimental.pallas import tpu as pltpu
from jax.sharding import PartitionSpec as P

MESH = pl.DeviceIdType.MESH
F32, BF16 = jnp.float32, jnp.bfloat16
NE = 12
NL = 4
NA = 3
NQ = 4
MT = 512
PT = 256


def gelu(c):
    return c * (0.5 * (1.0 + jnp.tanh(0.7978845608028654 * (c + 0.044715 * (c * c * c)))))


def kernel(x, w1, w2, out, ap, bo, bp, co, cp, g0, eo, ep,
           xg, he, hl, w1s, w1d, w2s, w2l, zs, ry, zo,
           lsem, lw, lv, lu, xs, xr, ws, wr, ys, yr, zys, zyr,
           ds, dr, fs, fr):
    cz, cy, cx = lax.axis_index('cz'), lax.axis_index('cy'), lax.axis_index('cx')
    X, Y, D = {'cy': 1 - cy}, {'cz': 1 - cz}, {'cx': 1 - cx}
    R, K = x.shape
    B1 = w1.shape[1]
    WC = B1 // (NE + NL)
    EC, LC = NE * WC, NL * WC
    C2 = w2.shape[1]
    QC = 2 * C2 // NQ

    def remote(src, dst, s, r, dev):
        return pltpu.make_async_remote_copy(src, dst, s, r, device_id=dev, device_id_type=MESH)

    barrier = pltpu.get_barrier_semaphore()
    for dev in (X, Y, D):
        pl.semaphore_signal(barrier, inc=1, device_id=dev, device_id_type=MESH)
    pl.semaphore_wait(barrier, 3)

    own, oth = pl.ds(0, R), pl.ds(R, R)
    klo, khi = pl.ds(0, K), pl.ds(K, K)

    x_x = remote(x, xg.at[own, khi], xs.at[0], xr.at[0], X)
    y_x = remote(x, xg.at[oth, klo], ys, yr.at[0], Y)
    y_xf = remote(xg.at[own, khi], xg.at[oth, khi], ys, yr.at[1], Y)
    y_w1 = remote(w1.at[:, pl.ds(EC, LC)], co, ys, yr.at[2], Y)

    def y_w2(b):
        return remote(w2.at[pl.ds(b * B1 + EC, LC), :], eo.at[b], ys, yr.at[3], Y)

    l_x = pltpu.make_async_copy(x, xg.at[own, klo], lsem.at[0])
    d_w1 = remote(w1, ap, ds.at[0], dr.at[0], D)
    d_w2 = remote(w2, g0, ds.at[1], dr.at[1], D)
    d_co = remote(co, cp, ds.at[2], dr.at[2], D)
    d_eo = remote(eo, ep, ds.at[3], dr.at[3], D)

    def chunk(j):
        return pl.ds(j * WC if isinstance(j, int) else pl.multiple_of(j * WC, WC), WC)

    lo_c, hi_c = pl.ds(0, WC), pl.ds(WC, WC)

    def x_w1(j):
        dst = w1d.at[0, :, lo_c] if isinstance(j, int) and j == NE - 1 else bo.at[j]
        return remote(w1.at[:, chunk(j)], dst, ws, wr.at[j], X)

    def x_co(k):
        return remote(co.at[:, chunk(k)], bo.at[NE + NL + k], ws, wr.at[NE + NL + k], X)

    def turn(j):
        return j % 2 if isinstance(j, int) else lax.rem(j, 2)

    def f_w1(j):
        return remote(bo.at[j], bp.at[j], fs, fr.at[turn(j)], D)

    f_last = remote(w1d.at[0, :, lo_c], w1d.at[0, :, hi_c], fs, fr.at[turn(NE - 1)], D)
    HC = WC // 2

    def part(h, other=0):
        return pl.ds((2 * h + other) * HC, HC)

    def cols_last(h):
        return pl.ds((NL - 1) * WC + h * HC, HC)

    def x_part(h):
        return remote(co.at[:, cols_last(h)], w1d.at[1, :, part(h)], ws, wr.at[NE + 2 * NL - 1 + h], X)

    def f_part(h):
        return remote(w1d.at[1, :, part(h)], w1d.at[1, :, part(h, 1)], fs, fr.at[turn(NE + 2 * NL - 1 + h)], D)

    def quads(s, j, first, second):
        return [pltpu.make_async_copy(src, w1s.at[s, rows, pl.ds(c * WC, WC)], lw.at[s, i])
                for src, rows, c, i in (
                    (first, klo, 0, 0), (second, klo, 1, 0), (bo.at[j], khi, 0, 1), (bp.at[j], khi, 1, 2))]

    def wait_tiles(s, i):
        if i == 0:
            pltpu.make_async_copy(w1.at[:, pl.ds(0, 2 * WC)], w1s.at[s, klo, :], lw.at[s, 0]).wait()
        else:
            pltpu.make_async_copy(bo.at[0], w1s.at[s, khi, pl.ds((i - 1) * WC, WC)], lw.at[s, i]).wait()

    def wait_w2s(q):
        pltpu.make_async_copy(w2.at[pl.ds(0, 2 * EC), pl.ds(0, QC)], w2s.at[q % 2], lv.at[q % 2]).wait()

    def wait_w2l(s):
        pltpu.make_async_copy(w1.at[pl.ds(0, 2 * WC), pl.ds(0, 2 * C2)], w2l.at[s], lu.at[s]).wait()

    def quads_near(s, j):
        return quads(s, j, w1.at[:, chunk(j)], ap.at[:, chunk(j)])

    def quads_far(s, k):
        return quads(s, NE + NL + k, co.at[:, chunk(k)], cp.at[:, chunk(k)])

    base = (pl.multiple_of(cx * B1, B1), pl.multiple_of((1 - cx) * B1, B1))

    def loads(q):
        src, c = (w2, q) if q < NQ // 2 else (g0, q - NQ // 2)
        return [pltpu.make_async_copy(src.at[pl.ds(base[b], EC), pl.ds(c * QC, QC)],
                                      w2s.at[q % 2, pl.ds(b * EC, EC), :], lv.at[q % 2]) for b in range(2)]

    def late_near(s, k):
        got = []
        for b in range(2):
            rows = pl.ds(pl.multiple_of(base[b] + EC + k * WC, WC), WC)
            for c, src in enumerate((w2, g0)):
                got.append(pltpu.make_async_copy(
                    src.at[rows, :], w2l.at[s, pl.ds(b * WC, WC), pl.ds(c * C2, C2)], lu.at[s]))
        return got

    def late_far(s, k):
        got = []
        for b, blk in enumerate((cx, 1 - cx)):
            for c, src in enumerate((eo, ep)):
                got.append(pltpu.make_async_copy(
                    src.at[blk, chunk(k), :], w2l.at[s, pl.ds(b * WC, WC), pl.ds(c * C2, C2)], lu.at[s]))
        return got

    NP = R // MT

    def z_y(q, i, n=MT):
        rows = pl.ds(i * n if isinstance(i, int) else pl.multiple_of(i * n, n), n)
        return remote(zs.at[q, rows, :], ry.at[q, rows, :], zys.at[0 if q < 2 else 1], zyr.at[0 if q < NQ - 1 else 1 + i], Y)

    def layer1(dst, col, row0, rows, s, half):
        @pl.loop(0, rows // MT)
        def _(i):
            r = pl.multiple_of(i * MT, MT)
            c = jnp.dot(xg[pl.ds(row0 + r, MT), :], w1s[s, :, pl.ds(half * WC, WC)], preferred_element_type=F32)
            dst[pl.ds(row0 + r, MT), pl.ds(col, WC)] = gelu(c.astype(BF16).astype(F32)).astype(BF16)

    def layer1d(dst, col, row0, rows, s, half, i):
        lanes = pl.ds(half * WC, WC)

        @pl.loop(0, rows // MT)
        def _(n):
            r = pl.ds(pl.multiple_of(row0 + n * MT, MT), MT)
            c = (jnp.dot(xg[r, klo], w1s[s, klo, lanes], preferred_element_type=F32)
                 + jnp.dot(xg[r, khi], w1d[i, :, lanes], preferred_element_type=F32))
            dst[r, pl.ds(col, WC)] = gelu(c.astype(BF16).astype(F32)).astype(BF16)

    def step(j):
        s = lax.rem(j, 2)
        q = quads_near(s, j)
        q[0].start()
        q[1].start()
        x_w1(j).wait_recv()
        f_w1(j).start()
        q[2].start()
        wait_tiles(s, 0)
        wait_tiles(s, 1)
        layer1(he, col(j, 0), 0, R, s, 0)
        f_w1(j).wait_recv()
        q[3].start()
        wait_tiles(s, 2)
        layer1(he, col(j, 1), 0, R, s, 1)

    def col(j, half):
        return half * EC + j * WC if isinstance(j, int) else pl.multiple_of(half * EC + j * WC, WC)

    x_x.start()
    y_x.start()
    l_x.start()
    for j in range(NE):
        x_w1(j).start()
    d_w1.start()
    d_w2.start()
    for q in range(2):
        for c in loads(q):
            c.start()

    x_x.wait_recv()
    y_xf.start()
    y_w1.start()
    y_w2(0).start()
    y_w2(1).start()
    l_x.wait()
    d_w1.wait_recv()

    @pl.loop(0, NA)
    def _(j):
        step(j)

    y_x.wait_recv()
    y_xf.wait_recv()

    for n, j in enumerate((2, 1, 0)):
        if n == 2:
            for i in range(3):
                wait_tiles(0, i)
        for half in range(2):
            layer1(he, col(j, half), R, R, j % 2, half)
        if n == 0:
            for c in quads_near(0, 0):
                c.start()
        if n == 1:
            for c in quads_near(NA % 2, NA)[:2]:
                c.start()

    def early_second(j, s):
        wait_tiles(s, 2)
        layer1(he, col(j, 1), 0, 2 * R, s, 1)

    def early(lo, hi):
        @pl.loop(lo, hi)
        def _(j):
            s = lax.rem(j, 2)
            x_w1(j).wait_recv()
            f_w1(j).start()
            q = quads_near(s, j)
            q[2].start()
            if lo == NA:
                @pl.when(j > lo)
                def _():
                    early_second(j - 1, 1 - s)
            else:
                early_second(j - 1, 1 - s)
            for c in quads_near(1 - s, j + 1)[:2]:
                c.start()
            wait_tiles(s, 0)
            wait_tiles(s, 1)
            layer1(he, col(j, 0), 0, 2 * R, s, 0)
            f_w1(j).wait_recv()
            q[3].start()

    early(NA, 8)
    y_w1.wait_recv()
    for k in range(NL):
        x_w1(NE + k).start()
    for k in range(NL - 1):
        x_co(k).start()
    x_part(0).start()
    x_part(1).start()
    d_co.start()
    early(8, 9)

    def z_part(lo, hi, first):
        lanes = [pl.ds(b * EC + lo * WC, (hi - lo) * WC) for b in range(2)]

        @pl.loop(0, NP)
        def _(i):
            r = pl.multiple_of(i * MT, MT)
            z = sum(jnp.dot(he[pl.ds(R + r, MT), l], w2s[0, l, :], preferred_element_type=F32) for l in lanes)
            zs[0, pl.ds(r, MT), :] = z if first else zs[0, pl.ds(r, MT), :] + z

    d_w2.wait_recv()
    wait_w2s(0)
    wait_w2s(1)
    z_part(0, 8, True)
    early(9, NE - 2)
    early_second(NE - 3, (NE - 3) % 2)
    j, s = NE - 2, (NE - 2) % 2
    x_w1(j).wait_recv()
    f_w1(j).start()
    q = quads_near(s, j)
    q[2].start()
    for c in quads_near(1 - s, j + 1)[:2]:
        c.start()
    wait_tiles(s, 0)
    wait_tiles(s, 1)
    layer1(he, col(j, 0), 0, 2 * R, s, 0)
    f_w1(j).wait_recv()
    q[3].start()
    early_second(j, s)
    z_part(8, NE - 1, False)
    PC = EC - WC

    j, s = NE - 1, (NE - 1) % 2
    wait_tiles(s, 0)

    @pl.loop(0, NP)
    def _(i):
        r = pl.multiple_of(i * MT, MT)
        zo[pl.ds(r, MT), pl.ds(0, 2 * WC)] = jnp.dot(
            xg[pl.ds(R + r, MT), klo], w1s[s, klo, :], preferred_element_type=F32)

    x_w1(j).wait_recv()
    f_last.start()

    @pl.loop(0, R // PT)
    def _(i):
        r = pl.multiple_of(i * PT, PT)

        def half_chunk(half):
            lanes = pl.ds(half * WC, WC)
            c = zo[pl.ds(r, PT), lanes] + jnp.dot(
                xg[pl.ds(R + r, PT), khi], w1d[0, :, lanes], preferred_element_type=F32)
            he[pl.ds(R + r, PT), pl.ds(col(j, half), WC)] = gelu(c.astype(BF16).astype(F32)).astype(BF16)

        half_chunk(0)

        @pl.when(i == 0)
        def _():
            f_last.wait_recv()

        half_chunk(1)
        zs[0, pl.ds(r, PT), :] = zs[0, pl.ds(r, PT), :] + (
            jnp.dot(he[pl.ds(R + r, PT), pl.ds(PC, WC)], w2s[0, pl.ds(PC, WC), :], preferred_element_type=F32)
            + jnp.dot(he[pl.ds(R + r, PT), pl.ds(EC + PC, WC)], w2s[0, pl.ds(EC + PC, WC), :], preferred_element_type=F32))
        z_y(0, i, PT).start()

    def z_other(q):
        @pl.loop(0, NP)
        def _(i):
            r = pl.multiple_of(i * MT, MT)
            zs[q, pl.ds(r, MT), :] = jnp.dot(he[pl.ds(R + r, MT), :], w2s[q % 2], preferred_element_type=F32)
            z_y(q, i).start()

    def z_own(q):
        @pl.loop(0, NP)
        def _(i):
            r = pl.ds(pl.multiple_of(i * MT, MT), MT)
            zo[r, pl.ds(q * QC, QC)] = jnp.dot(he[r, :], w2s[q % 2], preferred_element_type=F32)

    layer1d(he, col(j, 0), 0, R, s, 0, 0)
    layer1d(he, col(j, 1), 0, R, s, 1, 0)
    for q in range(NQ):
        if q:
            if q >= 2:
                wait_w2s(q)
            z_other(q)
        z_own(q)
        if q + 2 < NQ:
            for c in loads(q + 2):
                c.start()
        if q == 0:
            remote(eo, eo, ys, yr.at[3], Y).wait_recv()
            d_eo.start()

    d_co.wait_recv()
    d_eo.wait_recv()

    def second(s):
        wait_tiles(s, 2)
        layer1(hl, WC, 0, R, s, 1)
        layer2(s)

    def layer2(s):
        wait_w2l(s)

        @pl.loop(0, NP)
        def _(i):
            r = pl.ds(pl.multiple_of(i * MT, MT), MT)
            zo[r, :] = zo[r, :] + jnp.dot(hl[r, :], w2l[s], preferred_element_type=F32)

    def late_step(near, k, s, before):
        off = NE if near else NE + NL
        quad = quads_near(s, NE + k) if near else quads_far(s, k)
        for c in quad[:2] + (late_near(s, k) if near else late_far(s, k)):
            c.start()
        (x_w1(NE + k) if near else x_co(k)).wait_recv()
        f = f_w1(off + k)
        f.start()
        quad[2].start()
        before()
        wait_tiles(s, 0)
        wait_tiles(s, 1)
        layer1(hl, 0, 0, R, s, 0)
        f.wait_recv()
        quad[3].start()

    @pl.loop(0, NL)
    def _(k):
        s = lax.rem(NE + k, 2)

        def before():
            @pl.when(k > 0)
            def _():
                second(1 - s)

        late_step(True, k, s, before)

    @pl.loop(0, NL - 2)
    def _(k):
        s = lax.rem(NE + NL + k, 2)
        late_step(False, k, s, lambda: second(1 - s))

    k, s = NL - 2, (NE + 2 * NL - 2) % 2
    second(1 - s)
    late_step(False, k, s, lambda: None)
    s = 1 - s
    for h in range(2):
        for o, (wk, blk) in enumerate(((co, cx), (cp, 1 - cx))):
            pltpu.make_async_copy(wk.at[:, cols_last(h)], w1s.at[s, klo, part(h, o)], lw.at[s, 0]).start()
            for c, src in enumerate((eo, ep)):
                pltpu.make_async_copy(src.at[blk, cols_last(h), :],
                                      w2l.at[s, part(h, o), pl.ds(c * C2, C2)], lu.at[s]).start()

    def sent(n):
        two = pl.ds(2 * n, 2)
        return remote(zs.at[two], ry.at[two], zys.at[n], zyr.at[0], Y)

    wait_tiles(1 - s, 2)
    layer1(hl, WC, 0, R, 1 - s, 1)
    x_part(0).wait_recv()
    f_part(0).start()
    layer2(1 - s)
    sent(0).wait_send()
    wait_tiles(s, 0)
    f_part(0).wait_recv()
    layer1d(hl, 0, 0, R, s, 0, 1)
    wait_w2l(s)

    @pl.loop(0, NP)
    def _(i):
        r = pl.ds(pl.multiple_of(i * MT, MT), MT)
        zo[r, :] = zo[r, :] + jnp.dot(hl[r, lo_c], w2l[s, lo_c, :], preferred_element_type=F32)

    @pl.loop(0, NP)
    def _(i):
        r = pl.ds(pl.multiple_of(i * MT, MT), MT)
        zs[0, r, :] = jnp.dot(xg[r, klo], w1s[s, klo, hi_c], preferred_element_type=F32)

    x_part(1).wait_recv()
    f_part(1).start()
    f_part(1).wait_recv()
    @pl.loop(0, NP)
    def _(i):
        r = pl.ds(pl.multiple_of(i * MT, MT), MT)
        c = zs[0, r, :] + jnp.dot(xg[r, khi], w1d[1, :, hi_c], preferred_element_type=F32)
        hl[r, hi_c] = gelu(c.astype(BF16).astype(F32)).astype(BF16)

    def finish(q, i):
        r, l = pl.ds(i * MT, MT), pl.ds(q * QC, QC)
        half, c = divmod(q, NQ // 2)
        lanes = pl.multiple_of((1 - cx if half else cx) * C2 + c * QC, QC)
        z = zo[r, l] + jnp.dot(hl[r, hi_c], w2l[s, hi_c, l], preferred_element_type=F32)
        out[r, pl.ds(lanes, QC)] = (z + ry[q, r, :]).astype(BF16)

    few = pl.ds(0, NQ - 1)
    remote(zs.at[few], ry.at[few], zys.at[0], zyr.at[0], Y).wait_recv()
    for q in range(NQ - 1):
        for i in range(NP):
            finish(q, i)
    for i in range(NP):
        z_y(NQ - 1, i).wait_recv()
        finish(NQ - 1, i)
    sent(1).wait_send()
    remote(bo, bp, ws, wr.at[0], X).wait_send()
    remote(bo, bp, fs, fr.at[0], D).wait_send()
    remote(w1, ap, ys, yr.at[0], Y).wait_send()
    for c in (x_x, d_w1, d_w2, d_co, d_eo):
        c.wait_send()


def solution(mesh):
    data_spec = P(('dp', 'cx', 'cz'), 'cy')
    up_spec = P('cy', ('cz', 'cx'))
    down_spec = P('cz', ('cy', 'cx'))

    def local_mlp(x, w1, w2):
        R, K = x.shape
        B1 = w1.shape[1]
        WC = B1 // (NE + NL)
        EC, LC = NE * WC, NL * WC
        C2 = w2.shape[1]
        QC = 2 * C2 // NQ
        NX = NE + 2 * NL
        dma = pltpu.SemaphoreType.DMA
        any_spec = pl.BlockSpec(memory_space=pl.ANY)
        sds = jax.ShapeDtypeStruct
        outs = (
            pltpu.VMEM((R, K), BF16),
            sds(w1.shape, BF16),
            sds((NX, K, WC), BF16),
            sds((NX, K, WC), BF16),
            sds((K, LC), BF16),
            sds((K, LC), BF16),
            sds(w2.shape, BF16),
            sds((2, LC, C2), BF16),
            sds((2, LC, C2), BF16),
        )
        scratch = [
            pltpu.VMEM((2 * R, 2 * K), BF16),
            pltpu.VMEM((2 * R, 2 * EC), BF16),
            pltpu.VMEM((R, 2 * WC), BF16),
            pltpu.VMEM((2, 2 * K, 2 * WC), BF16),
            pltpu.VMEM((2, K, 2 * WC), BF16),
            pltpu.VMEM((2, 2 * EC, QC), BF16),
            pltpu.VMEM((2, 2 * WC, 2 * C2), BF16),
            pltpu.VMEM((NQ, R, QC), F32),
            pltpu.VMEM((NQ, R, QC), F32),
            pltpu.VMEM((R, 2 * C2), F32),
            dma((1,)), dma((2, 3)), dma((2,)), dma((2,)),
            dma((1,)), dma((1,)),
            dma, dma((NX + 1,)),
            dma, dma((4,)),
            dma((2,)), dma((1 + R // MT,)),
            dma((4,)), dma((4,)),
            dma, dma((2,)),
        ]
        return pl.pallas_call(
            kernel,
            out_shape=outs,
            in_specs=[any_spec] * 3,
            out_specs=(pl.BlockSpec(memory_space=pltpu.VMEM),) + (any_spec,) * (len(outs) - 1),
            scratch_shapes=scratch,
            compiler_params=pltpu.CompilerParams(
                collective_id=0, has_side_effects=True, vmem_limit_bytes=67043328 - 2 * R * K),
            name='mlp',
        )(x, w1, w2)[0]

    return jax.shard_map(local_mlp, mesh=mesh, in_specs=(data_spec, up_spec, down_spec), out_specs=data_spec, check_vma=False)
```

profile of v0, /device:TPU:0, one launch (start us, length us, event | category | flops | bytes accessed | tf_op | source)
XLA Modules:
  0.0 280.5 jit_solution(124775097019666347)
XLA Ops:
  0.0 279.2 %mlp.1 = (bf16[1024,1024]{1,0:T(8,128)(2,1)S(1)}, bf16[1024,4096]{1,0:T(8,128)(2,1)}, bf16[20,1024,256]{2,1,0:T(8,128)(2,1)}, bf16[20,1024,256]{2,1,0:T(8,128)(2...) custom-call(bf16[1024,1024]{1,0:T(8,128)(2,1)} %x.1, ...), custom_call_target="tpu_custom_call" | custom-call | tf_op jit(solution)/shard_map/mlp/pallas_call | solution.py:513
  279.2 1.3 copy.5
where the time goes:
time: 281 us
  Pallas kernels  279 us (99%)
    pallas_call x1, Pallas kernels, local_mlp(): pl.pallas_call(kernel, out_shape=outs, in_specs=[any_spec] * 3, out_specs...  279 us

commit v1 on v0

--- a/solution.py
+++ b/solution.py
@@ -12,7 +12,7 @@
 NA = 3
 NQ = 4
 MT = 512
-PT = 256
+PT = 128
 
 
 def gelu(c):
@@ -427,13 +427,18 @@
         r = pl.ds(pl.multiple_of(i * MT, MT), MT)
         zo[r, :] = zo[r, :] + jnp.dot(hl[r, lo_c], w2l[s, lo_c, :], preferred_element_type=F32)
 
+    def take():
+        x_part(1).wait_recv()
+        f_part(1).start()
+
+    pl.when(cx == 1)(take)
+
     @pl.loop(0, NP)
     def _(i):
         r = pl.ds(pl.multiple_of(i * MT, MT), MT)
         zs[0, r, :] = jnp.dot(xg[r, klo], w1s[s, klo, hi_c], preferred_element_type=F32)
-
-    x_part(1).wait_recv()
-    f_part(1).start()
+        pl.when((cx == 0) & (i == 0))(take)
+
     f_part(1).wait_recv()
     @pl.loop(0, NP)
     def _(i):

time: 281 us -> 281 us (level)
  no operation moved by 1% of the time
where the time goes in v1:
time: 281 us; the launch traced here: 280 us
  Pallas kernels  279 us (99%)
    pallas_call x1, Pallas kernels, local_mlp(): pl.pallas_call(kernel, out_shape=outs, in_specs=[any_spec] * 3, out_specs...  279 us

profile of v1, /device:TPU:0, one launch (start us, length us, event | category | flops | bytes accessed | tf_op | source)
XLA Modules:
  0.0 280.1 jit_solution(4389442053860954696)
XLA Ops:
  0.0 278.8 %mlp.1 = (bf16[1024,1024]{1,0:T(8,128)(2,1)S(1)}, bf16[1024,4096]{1,0:T(8,128)(2,1)}, bf16[20,1024,256]{2,1,0:T(8,128)(2,1)}, bf16[20,1024,256]{2,1,0:T(8,128)(2...) custom-call(bf16[1024,1024]{1,0:T(8,128)(2,1)} %x.1, ...), custom_call_target="tpu_custom_call" | custom-call | tf_op jit(solution)/shard_map/mlp/pallas_call | solution.py:518
  278.8 1.3 copy.5

commit v2 on v1

--- a/solution.py
+++ b/solution.py
@@ -13,6 +13,7 @@
 NQ = 4
 MT = 512
 PT = 128
+SP = 128
 
 
 def gelu(c):
@@ -25,6 +26,7 @@
            ds, dr, fs, fr):
     cz, cy, cx = lax.axis_index('cz'), lax.axis_index('cy'), lax.axis_index('cx')
     X, Y, D = {'cy': 1 - cy}, {'cz': 1 - cz}, {'cx': 1 - cx}
+    XD = {'cy': 1 - cy, 'cx': 1 - cx}
     R, K = x.shape
     B1 = w1.shape[1]
     WC = B1 // (NE + NL)
@@ -36,9 +38,9 @@
         return pltpu.make_async_remote_copy(src, dst, s, r, device_id=dev, device_id_type=MESH)
 
     barrier = pltpu.get_barrier_semaphore()
-    for dev in (X, Y, D):
+    for dev in (X, Y, D, XD):
         pl.semaphore_signal(barrier, inc=1, device_id=dev, device_id_type=MESH)
-    pl.semaphore_wait(barrier, 3)
+    pl.semaphore_wait(barrier, 4)
 
     own, oth = pl.ds(0, R), pl.ds(R, R)
     klo, khi = pl.ds(0, K), pl.ds(K, K)
@@ -63,8 +65,13 @@
     lo_c, hi_c = pl.ds(0, WC), pl.ds(WC, WC)
 
     def x_w1(j):
-        dst = w1d.at[0, :, lo_c] if isinstance(j, int) and j == NE - 1 else bo.at[j]
-        return remote(w1.at[:, chunk(j)], dst, ws, wr.at[j], X)
+        return remote(w1.at[:, chunk(j)], bo.at[j], ws, wr.at[j], X)
+
+    head, tail = pl.ds(0, K - SP), pl.ds(K - SP, SP)
+    x_head = remote(w1.at[head, chunk(NE - 1)], w1d.at[0, head, lo_c], xs.at[1], wr.at[NE - 1], X)
+
+    def x_tail(src, dev):
+        return remote(src.at[tail, chunk(NE - 1)], w1d.at[0, tail, lo_c], xs.at[2], wr.at[NE + 2 * NL + 1], dev)
 
     def x_co(k):
         return remote(co.at[:, chunk(k)], bo.at[NE + NL + k], ws, wr.at[NE + NL + k], X)
@@ -182,8 +189,14 @@
     x_x.start()
     y_x.start()
     l_x.start()
-    for j in range(NE):
+    for j in range(NE - 1):
         x_w1(j).start()
+    x_head.start()
+
+    @pl.when(cx == 1)
+    def _():
+        x_tail(w1, X).start()
+
     d_w1.start()
     d_w2.start()
     for q in range(2):
@@ -197,6 +210,11 @@
     y_w2(1).start()
     l_x.wait()
     d_w1.wait_recv()
+
+    @pl.when(cx == 1)
+    def _():
+        x_tail(ap, XD).start()
+
 
     @pl.loop(0, NA)
     def _(j):
@@ -295,7 +313,8 @@
         zo[pl.ds(r, MT), pl.ds(0, 2 * WC)] = jnp.dot(
             xg[pl.ds(R + r, MT), klo], w1s[s, klo, :], preferred_element_type=F32)
 
-    x_w1(j).wait_recv()
+    x_head.wait_recv()
+    x_tail(w1, X).wait_recv()
     f_last.start()
 
     @pl.loop(0, R // PT)
@@ -462,7 +481,15 @@
         z_y(NQ - 1, i).wait_recv()
         finish(NQ - 1, i)
     sent(1).wait_send()
-    remote(bo, bp, ws, wr.at[0], X).wait_send()
+    most = pl.ds(0, NE + 2 * NL - 1)
+    remote(bo.at[most], bp.at[most], ws, wr.at[0], X).wait_send()
+    x_head.wait_send()
+
+    @pl.when(cx == 1)
+    def _():
+        both = pl.ds(0, 2 * SP)
+        remote(w1.at[both, chunk(0)], w1d.at[0, both, lo_c], xs.at[2], wr.at[0], X).wait_send()
+
     remote(bo, bp, fs, fr.at[0], D).wait_send()
     remote(w1, ap, ys, yr.at[0], Y).wait_send()
     for c in (x_x, d_w1, d_w2, d_co, d_eo):
@@ -508,8 +535,8 @@
             pltpu.VMEM((NQ, R, QC), F32),
             pltpu.VMEM((R, 2 * C2), F32),
             dma((1,)), dma((2, 3)), dma((2,)), dma((2,)),
-            dma((1,)), dma((1,)),
-            dma, dma((NX + 1,)),
+            dma((3,)), dma((1,)),
+            dma, dma((NX + 2,)),
             dma, dma((4,)),
             dma((2,)), dma((1 + R // MT,)),
             dma((4,)), dma((4,)),

time: 281 us -> 281 us (level)
  no operation moved by 1% of the time
where the time goes in v2:
time: 281 us; the launch traced here: 280 us
  Pallas kernels  279 us (99%)
    pallas_call x1, Pallas kernels, local_mlp(): pl.pallas_call(kernel, out_shape=outs, in_specs=[any_spec] * 3, out_specs...  279 us

profile of v2, /device:TPU:0, one launch (start us, length us, event | category | flops | bytes accessed | tf_op | source)
XLA Modules:
  0.0 280.4 jit_solution(16664361644047511283)
XLA Ops:
  0.0 279.1 %mlp.1 = (bf16[1024,1024]{1,0:T(8,128)(2,1)S(1)}, bf16[1024,4096]{1,0:T(8,128)(2,1)}, bf16[20,1024,256]{2,1,0:T(8,128)(2,1)}, bf16[20,1024,256]{2,1,0:T(8,128)(2...) custom-call(bf16[1024,1024]{1,0:T(8,128)(2,1)} %x.1, ...), custom_call_target="tpu_custom_call" | custom-call | tf_op jit(solution)/shard_map/mlp/pallas_call | solution.py:545
  279.1 1.3 copy.5

commit v3 on v2

--- a/solution.py
+++ b/solution.py
@@ -289,18 +289,34 @@
     early(9, NE - 2)
     early_second(NE - 3, (NE - 3) % 2)
     j, s = NE - 2, (NE - 2) % 2
+    q = quads_near(s, j)
+
+    def theirs():
+        f_w1(j).wait_recv()
+        q[3].start()
+
+    pl.when(cx == 0)(theirs)
     x_w1(j).wait_recv()
     f_w1(j).start()
-    q = quads_near(s, j)
     q[2].start()
     for c in quads_near(1 - s, j + 1)[:2]:
         c.start()
     wait_tiles(s, 0)
-    wait_tiles(s, 1)
-    layer1(he, col(j, 0), 0, 2 * R, s, 0)
-    f_w1(j).wait_recv()
-    q[3].start()
-    early_second(j, s)
+
+    def half_of(half):
+        pltpu.make_async_copy(bo.at[0], w1s.at[s, khi, lo_c], lw.at[s, 1 + half]).wait()
+        lanes = pl.ds(pl.multiple_of(half * WC, WC), WC)
+        cols = pl.ds(pl.multiple_of(half * EC + j * WC, WC), WC)
+
+        @pl.loop(0, 2 * NP)
+        def _(i):
+            r = pl.ds(pl.multiple_of(i * MT, MT), MT)
+            c = jnp.dot(xg[r, :], w1s[s, :, lanes], preferred_element_type=F32)
+            he[r, cols] = gelu(c.astype(BF16).astype(F32)).astype(BF16)
+
+    half_of(1 - cx)
+    pl.when(cx == 1)(theirs)
+    half_of(cx)
     z_part(8, NE - 1, False)
     PC = EC - WC
 

time: 281 us -> 281 us (level)
  no operation moved by 1% of the time
where the time goes in v3:
time: 281 us; the launch traced here: 280 us
  Pallas kernels  279 us (99%)
    pallas_call x1, Pallas kernels, local_mlp(): pl.pallas_call(kernel, out_shape=outs, in_specs=[any_spec] * 3, out_specs...  279 us

profile of v3, /device:TPU:0, one launch (start us, length us, event | category | flops | bytes accessed | tf_op | source)
XLA Modules:
  0.0 280.4 jit_solution(174779274994797085)
XLA Ops:
  0.0 279.1 %mlp.1 = (bf16[1024,1024]{1,0:T(8,128)(2,1)S(1)}, bf16[1024,4096]{1,0:T(8,128)(2,1)}, bf16[20,1024,256]{2,1,0:T(8,128)(2,1)}, bf16[20,1024,256]{2,1,0:T(8,128)(2...) custom-call(bf16[1024,1024]{1,0:T(8,128)(2,1)} %x.1, ...), custom_call_target="tpu_custom_call" | custom-call | tf_op jit(solution)/shard_map/mlp/pallas_call | solution.py:561
  279.1 1.3 copy.5

commit v4 on v1

--- a/solution.py
+++ b/solution.py
@@ -271,18 +271,34 @@
     early(9, NE - 2)
     early_second(NE - 3, (NE - 3) % 2)
     j, s = NE - 2, (NE - 2) % 2
+    q = quads_near(s, j)
+
+    def theirs():
+        f_w1(j).wait_recv()
+        q[3].start()
+
+    pl.when(cx == 0)(theirs)
     x_w1(j).wait_recv()
     f_w1(j).start()
-    q = quads_near(s, j)
     q[2].start()
     for c in quads_near(1 - s, j + 1)[:2]:
         c.start()
     wait_tiles(s, 0)
-    wait_tiles(s, 1)
-    layer1(he, col(j, 0), 0, 2 * R, s, 0)
-    f_w1(j).wait_recv()
-    q[3].start()
-    early_second(j, s)
+
+    def half_of(half):
+        pltpu.make_async_copy(bo.at[0], w1s.at[s, khi, lo_c], lw.at[s, 1 + half]).wait()
+        lanes = pl.ds(pl.multiple_of(half * WC, WC), WC)
+        cols = pl.ds(pl.multiple_of(half * EC + j * WC, WC), WC)
+
+        @pl.loop(0, 2 * NP)
+        def _(i):
+            r = pl.ds(pl.multiple_of(i * MT, MT), MT)
+            c = jnp.dot(xg[r, :], w1s[s, :, lanes], preferred_element_type=F32)
+            he[r, cols] = gelu(c.astype(BF16).astype(F32)).astype(BF16)
+
+    half_of(1 - cx)
+    pl.when(cx == 1)(theirs)
+    half_of(cx)
     z_part(8, NE - 1, False)
     PC = EC - WC
 

time: 281 us -> 281 us (level)
  no operation moved by 1% of the time
where the time goes in v4:
time: 281 us; the launch traced here: 280 us
  Pallas kernels  279 us (99%)
    pallas_call x1, Pallas kernels, local_mlp(): pl.pallas_call(kernel, out_shape=outs, in_specs=[any_spec] * 3, out_specs...  279 us

profile of v4, /device:TPU:0, one launch (start us, length us, event | category | flops | bytes accessed | tf_op | source)
XLA Modules:
  0.0 280.1 jit_solution(9261932108115630683)
XLA Ops:
  0.0 278.8 %mlp.1 = (bf16[1024,1024]{1,0:T(8,128)(2,1)S(1)}, bf16[1024,4096]{1,0:T(8,128)(2,1)}, bf16[20,1024,256]{2,1,0:T(8,128)(2,1)}, bf16[20,1024,256]{2,1,0:T(8,128)(2...) custom-call(bf16[1024,1024]{1,0:T(8,128)(2,1)} %x.1, ...), custom_call_target="tpu_custom_call" | custom-call | tf_op jit(solution)/shard_map/mlp/pallas_call | solution.py:534
  278.8 1.3 copy.5

commit v5 on v4

--- a/solution.py
+++ b/solution.py
@@ -13,6 +13,7 @@
 NQ = 4
 MT = 512
 PT = 128
+ET = 256
 
 
 def gelu(c):
@@ -341,7 +342,11 @@
         def _(i):
             r = pl.multiple_of(i * MT, MT)
             zs[q, pl.ds(r, MT), :] = jnp.dot(he[pl.ds(R + r, MT), :], w2s[q % 2], preferred_element_type=F32)
-            z_y(q, i).start()
+            if q < NQ - 1:
+                z_y(q, i).start()
+            else:
+                for n in range(MT // ET):
+                    z_y(q, i * (MT // ET) + n, ET).start()
 
     def z_own(q):
         @pl.loop(0, NP)
@@ -462,8 +467,8 @@
         c = zs[0, r, :] + jnp.dot(xg[r, khi], w1d[1, :, hi_c], preferred_element_type=F32)
         hl[r, hi_c] = gelu(c.astype(BF16).astype(F32)).astype(BF16)
 
-    def finish(q, i):
-        r, l = pl.ds(i * MT, MT), pl.ds(q * QC, QC)
+    def finish(q, i, n=MT):
+        r, l = pl.ds(i * n, n), pl.ds(q * QC, QC)
         half, c = divmod(q, NQ // 2)
         lanes = pl.multiple_of((1 - cx if half else cx) * C2 + c * QC, QC)
         z = zo[r, l] + jnp.dot(hl[r, hi_c], w2l[s, hi_c, l], preferred_element_type=F32)
@@ -474,9 +479,9 @@
     for q in range(NQ - 1):
         for i in range(NP):
             finish(q, i)
-    for i in range(NP):
-        z_y(NQ - 1, i).wait_recv()
-        finish(NQ - 1, i)
+    for i in range(R // ET):
+        z_y(NQ - 1, i, ET).wait_recv()
+        finish(NQ - 1, i, ET)
     sent(1).wait_send()
     remote(bo, bp, ws, wr.at[0], X).wait_send()
     remote(bo, bp, fs, fr.at[0], D).wait_send()
@@ -527,7 +532,7 @@
             dma((1,)), dma((1,)),
             dma, dma((NX + 1,)),
             dma, dma((4,)),
-            dma((2,)), dma((1 + R // MT,)),
+            dma((2,)), dma((1 + R // ET,)),
             dma((4,)), dma((4,)),
             dma, dma((2,)),
         ]

time: 281 us -> 281 us (level)
  no operation moved by 1% of the time
where the time goes in v5:
time: 281 us; the launch traced here: 280 us
  Pallas kernels  279 us (99%)
    pallas_call x1, Pallas kernels, local_mlp(): pl.pallas_call(kernel, out_shape=outs, in_specs=[any_spec] * 3, out_specs...  279 us

profile of v5, /device:TPU:0, one launch (start us, length us, event | category | flops | bytes accessed | tf_op | source)
XLA Modules:
  0.0 280.1 jit_solution(5619544086478455466)
XLA Ops:
  0.0 278.7 %mlp.1 = (bf16[1024,1024]{1,0:T(8,128)(2,1)S(1)}, bf16[1024,4096]{1,0:T(8,128)(2,1)}, bf16[20,1024,256]{2,1,0:T(8,128)(2,1)}, bf16[20,1024,256]{2,1,0:T(8,128)(2...) custom-call(bf16[1024,1024]{1,0:T(8,128)(2,1)} %x.1, ...), custom_call_target="tpu_custom_call" | custom-call | tf_op jit(solution)/shard_map/mlp/pallas_call | solution.py:539
  278.7 1.3 copy.5

commit v6 on v5

--- a/solution.py
+++ b/solution.py
@@ -461,11 +461,8 @@
         pl.when((cx == 0) & (i == 0))(take)
 
     f_part(1).wait_recv()
-    @pl.loop(0, NP)
-    def _(i):
-        r = pl.ds(pl.multiple_of(i * MT, MT), MT)
-        c = zs[0, r, :] + jnp.dot(xg[r, khi], w1d[1, :, hi_c], preferred_element_type=F32)
-        hl[r, hi_c] = gelu(c.astype(BF16).astype(F32)).astype(BF16)
+    c = zs[0] + jnp.dot(xg[own, khi], w1d[1, :, hi_c], preferred_element_type=F32)
+    hl[:, hi_c] = gelu(c.astype(BF16).astype(F32)).astype(BF16)
 
     def finish(q, i, n=MT):
         r, l = pl.ds(i * n, n), pl.ds(q * QC, QC)

time: 281 us -> 281 us (level)
  no operation moved by 1% of the time
where the time goes in v6:
time: 281 us
  Pallas kernels  279 us (99%)
    pallas_call x1, Pallas kernels, local_mlp(): pl.pallas_call(kernel, out_shape=outs, in_specs=[any_spec] * 3, out_specs...  279 us

profile of v6, /device:TPU:0, one launch (start us, length us, event | category | flops | bytes accessed | tf_op | source)
XLA Modules:
  0.0 280.6 jit_solution(18553387362250613)
XLA Ops:
  0.0 279.2 %mlp.1 = (bf16[1024,1024]{1,0:T(8,128)(2,1)S(1)}, bf16[1024,4096]{1,0:T(8,128)(2,1)}, bf16[20,1024,256]{2,1,0:T(8,128)(2,1)}, bf16[20,1024,256]{2,1,0:T(8,128)(2...) custom-call(bf16[1024,1024]{1,0:T(8,128)(2,1)} %x.1, ...), custom_call_target="tpu_custom_call" | custom-call | tf_op jit(solution)/shard_map/mlp/pallas_call | solution.py:536
  279.2 1.3 copy.5
